TPU v7x, 32 devices: a whole 2x2x4 slice. The times are simulated.
32 devices in a mesh: rows: 8 (over z, x), cols: 4 (over y, core).
Axes of the slice: x: 2, y: 2, z: 4, core: 2. Of those that a mesh axis runs over, the one named last changes fastest.
Arguments:
- panel: float32 [4096, 1024], P('rows'), as said below
- window_block: float32 [4096, 2048], P('rows', 'cols'), may hold values from -6 to 6
- row_live: int32 [8], replicated, may hold values 0 or 1
- window_rows: int32 [4], replicated, may hold values from 2 to 7, as said below
Outputs:
- factor: float32 [4096, 1024], P('rows')
- updated: float32 [4096, 2048], P('rows', 'cols')
Inputs may be any that keep to these rules, and one draw needn't show every extreme that they name: `window_rows`: distinct tile rows, none inside the supernode. `row_live`: the value for tile rows below 2 is ignored: those rows are always present. `panel`: the first 1024 rows hold a symmetric positive definite block.
All inputs are finite; a program needn't handle non-finite values.
Results may differ from a plain program's by a relative error of at most 0.0001.
Values sent between devices are 32-bit elements; how exact they have to be, the bound alone decides.
A program may use at most 128 MiB of HBM per device.

v0:
```python
import jax
import jax.numpy as jnp
from jax import lax
from jax.sharding import PartitionSpec as P

P_SIZE = 2


HIGHEST = lax.Precision.HIGHEST
CONTRACT = (((1,), (1,)), ((), ()))


def from_root(value, axis, source):
    kept = jnp.where(lax.axis_index(axis) == source, value, 0).astype(value.dtype)
    return lax.psum(kept, axis)


def times_trans(left, right):
    return lax.dot_general(left, right, CONTRACT, precision=HIGHEST)


def symmetric(square):
    return jnp.tril(square) + jnp.tril(square, -1).T


def factor_tile(square):
    lower_tile = jnp.linalg.cholesky(square)
    identity_tile = jnp.eye(square.shape[0], dtype=jnp.float32)
    inverse = lax.linalg.triangular_solve(lower_tile, identity_tile, left_side=True, lower=True)
    return (lower_tile, inverse)


def column(block, section, width):
    return block[:, section * width : (section + 1) * width]


def solve_row(block, super_rows, inverses, width):
    tiles_now = []
    for section in range(P_SIZE):
        update = column(block, section, width)
        for earlier in range(section):
            update = update - times_trans(tiles_now[earlier], super_rows[section][earlier])
        tiles_now.append(times_trans(update, inverses[section]))
    return jnp.concatenate(tiles_now, axis=1)


def shards(panel, window_block, row_live, window_rows):
    width = panel.shape[0]
    device_row = lax.axis_index("rows")
    device_col = lax.axis_index("cols")
    live_flag = jnp.where(device_row < P_SIZE, 1, row_live[device_row]).astype(jnp.float32)
    scaled = panel * live_flag
    target = window_rows[device_col]
    target_raw = from_root(scaled, "rows", target)
    own_tiles = []
    super_rows = []
    inverses = []
    identity_tile = jnp.eye(width, dtype=jnp.float32)
    for section in range(P_SIZE):
        square = symmetric(column(scaled, section, width))
        for earlier in range(section):
            square = square - times_trans(own_tiles[earlier], own_tiles[earlier])
        square = jnp.where(device_row == section, square, identity_tile)
        lower_tile, inverse = factor_tile(square)
        payload = jnp.concatenate(own_tiles + [inverse], axis=1)
        received = from_root(payload, "rows", section)
        earlier_tiles = [column(received, earlier, width) for earlier in range(section)]
        inverses.append(column(received, section, width))
        super_rows.append(earlier_tiles)
        update = column(scaled, section, width)
        for earlier in range(section):
            update = update - times_trans(own_tiles[earlier], earlier_tiles[earlier])
        solved = times_trans(update, inverses[section])
        solved = jnp.where(device_row == section, lower_tile, solved)
        solved = jnp.where(device_row < section, jnp.zeros_like(solved), solved)
        own_tiles.append(solved)
    own_row = jnp.concatenate(own_tiles, axis=1)
    target_row = solve_row(target_raw, super_rows, inverses, width)
    updated = window_block - times_trans(own_row, target_row)
    return (own_row, updated)


def solution(mesh):
    in_specs = (P("rows", None), P("rows", "cols"), P(), P())
    out_specs = (P("rows", None), P("rows", "cols"))
    return jax.shard_map(shards, mesh=mesh, in_specs=in_specs, out_specs=out_specs, check_vma=False)
```

profile of v0, /device:TPU:0, one launch (start us, length us, event | category | flops | bytes accessed | tf_op | source)
XLA Modules:
  0.0 616.8 jit_solution(17323084982662087415)
XLA Ops:
  12.1 3.6 broadcast_select_fusion
  23.6 11.7 %cholesky.286 = f32[128,128]{1,0:T(8,128)S(1)} custom-call(f32[128,128]{1,0:T(8,128)S(1)} %cholesky.426), custom_call_target="Cholesky" | custom-call | tf_op jit(solution)/shard_map/jit(cholesky)/cholesky | solution.py:27
  35.9 9.8 %custom-call.27 = f32[1,128,128]{1,2,0:T(8,128)S(1)} custom-call(f32[1,128,128]{2,1,0:T(8,128)S(1)} %get-tuple-element.65), custom_call_target="InvertDiagBlocksLowerTriangular" | custom-call | tf_op jit(solution)/shard_map/jit(cholesky)/cholesky | solution.py:27
  48.6 12.8 %cholesky.305 = f32[128,128]{1,0:T(8,128)} custom-call(f32[128,128]{1,0:T(8,128)S(1)} %cholesky.430), custom_call_target="Cholesky" | custom-call | tf_op jit(solution)/shard_map/jit(cholesky)/cholesky | solution.py:27
  63.3 9.8 %custom-call.28 = f32[1,128,128]{1,2,0:T(8,128)S(1)} custom-call(f32[1,128,128]{2,1,0:T(8,128)S(1)} %get-tuple-element.62), custom_call_target="InvertDiagBlocksLowerTriangular" | custom-call | tf_op jit(solution)/shard_map/jit(cholesky)/cholesky | solution.py:27
  74.7 11.7 %cholesky.326 = f32[128,128]{1,0:T(8,128)S(1)} custom-call(f32[128,128]{1,0:T(8,128)S(1)} %cholesky.435), custom_call_target="Cholesky" | custom-call | tf_op jit(solution)/shard_map/jit(cholesky)/cholesky | solution.py:27
  87.1 9.8 %custom-call.29 = f32[1,128,128]{1,2,0:T(8,128)S(1)} custom-call(f32[1,128,128]{2,1,0:T(8,128)S(1)} %get-tuple-element.59), custom_call_target="InvertDiagBlocksLowerTriangular" | custom-call | tf_op jit(solution)/shard_map/jit(cholesky)/cholesky | solution.py:27
  98.3 11.9 %cholesky.343 = f32[128,128]{1,0:T(8,128)S(1)} custom-call(f32[128,128]{1,0:T(8,128)S(1)} %convolution_subtract_fusion.14), custom_call_target="Cholesky" | custom-call | tf_op jit(solution)/shard_map/jit(cholesky)/cholesky | solution.py:27
  115.3 11.9 %while.4 = (s32[]{:T(128)}, f32[512,512]{1,0:T(8,128)}, s32[4,2]{0,1:T(2,128)S(1)}, f32[4,128,128]{2,1,0:T(8,128)S(1)}, s32[]{:T(128)}) while((s32[]{:T(128)}, f32[512,512]{1,0:T(8,128)}, s32[4,2]{0,1:T(2,128)S(1)}, f32[4,128,128]{2,1,0:T(8,128)S(1)}, s32[]{:T(128)}) %tuple.55), condition=%wide.while_cond, body=%wide.while_body.sunk | while | flops 2 | bytes 131189 | solution.py:29
  116.0 2.3 bitcast_dynamic-update-slice_fusion.4
  128.0 40.1 %custom-call.30 = f32[4,128,128]{1,2,0:T(8,128)S(1)} custom-call(f32[4,128,128]{2,1,0:T(8,128)} %copy-done.15), custom_call_target="InvertDiagBlocksLowerTriangular" | custom-call | tf_op jit(solution)/shard_map/triangular_solve/custom-call.3 | solution.py:29
  174.0 2.4 convolution_subtract_fusion.8
  179.5 79.6 %all-reduce.5.cloned.1.call-done = f32[512,512]{1,0:T(8,128)} async-done(((f32[512,512]{1,0:T(8,128)}), f32[512,512]{1,0:T(8,128)}) %all-reduce.5.cloned.1.call-update) | async-done | bytes 1048592 | tf_op jit(solution)/shard_map/psum | solution.py:15
  259.2 3.6 fusion.10
  262.8 2.9 fusion.8
  265.7 2.6 copy.19
  271.1 11.7 %cholesky.358 = f32[128,128]{1,0:T(8,128)S(1)} custom-call(f32[128,128]{1,0:T(8,128)S(1)} %cholesky.439), custom_call_target="Cholesky" | custom-call | tf_op jit(solution)/shard_map/jit(cholesky)/cholesky | solution.py:27
  283.4 9.8 %custom-call.31 = f32[1,128,128]{1,2,0:T(8,128)S(1)} custom-call(f32[1,128,128]{2,1,0:T(8,128)S(1)} %get-tuple-element.55), custom_call_target="InvertDiagBlocksLowerTriangular" | custom-call | tf_op jit(solution)/shard_map/jit(cholesky)/cholesky | solution.py:27
  298.3 12.1 %cholesky.377 = f32[128,128]{1,0:T(8,128)S(1)} custom-call(f32[128,128]{1,0:T(8,128)S(1)} %cholesky.443), custom_call_target="Cholesky" | custom-call | tf_op jit(solution)/shard_map/jit(cholesky)/cholesky | solution.py:27
  314.4 9.8 %custom-call.32 = f32[1,128,128]{1,2,0:T(8,128)S(1)} custom-call(f32[1,128,128]{2,1,0:T(8,128)S(1)} %get-tuple-element.52), custom_call_target="InvertDiagBlocksLowerTriangular" | custom-call | tf_op jit(solution)/shard_map/jit(cholesky)/cholesky | solution.py:27
  327.5 11.7 %cholesky.398 = f32[128,128]{1,0:T(8,128)S(1)} custom-call(f32[128,128]{1,0:T(8,128)S(1)} %cholesky.448), custom_call_target="Cholesky" | custom-call | tf_op jit(solution)/shard_map/jit(cholesky)/cholesky | solution.py:27
  340.5 10.0 %custom-call.33 = f32[1,128,128]{1,2,0:T(8,128)S(1)} custom-call(f32[1,128,128]{2,1,0:T(8,128)S(1)} %get-tuple-element.49), custom_call_target="InvertDiagBlocksLowerTriangular" | custom-call | tf_op jit(solution)/shard_map/jit(cholesky)/cholesky | solution.py:27
  352.8 11.7 %cholesky.415 = f32[128,128]{1,0:T(8,128)S(1)} custom-call(f32[128,128]{1,0:T(8,128)S(1)} %convolution_subtract_fusion.13), custom_call_target="Cholesky" | custom-call | tf_op jit(solution)/shard_map/jit(cholesky)/cholesky | solution.py:27
  368.2 2.4 fusion.16
  370.6 11.7 %while.5 = (s32[]{:T(128)}, f32[512,512]{1,0:T(8,128)}, s32[4,2]{0,1:T(2,128)S(1)}, f32[4,128,128]{2,1,0:T(8,128)S(1)}, s32[]{:T(128)}) while((s32[]{:T(128)}, f32[512,512]{1,0:T(8,128)}, s32[4,2]{0,1:T(2,128)S(1)}, f32[4,128,128]{2,1,0:T(8,128)S(1)}, s32[]{:T(128)}) %tuple.66), condition=%wide.while_cond.clone, body=%wide.while_body.clone.sunk | while | flops 2 | bytes 131189 | solution.py:29
  383.0 40.3 %custom-call.34 = f32[4,128,128]{1,2,0:T(8,128)S(1)} custom-call(f32[4,128,128]{2,1,0:T(8,128)} %copy-done.14), custom_call_target="InvertDiagBlocksLowerTriangular" | custom-call | tf_op jit(solution)/shard_map/triangular_solve/custom-call.3 | solution.py:29
  429.2 2.4 convolution_subtract_fusion.7
  433.6 156.1 %all-reduce.7.cloned.1.call-done = (f32[512,1024]{1,0:T(8,128)}, f32[512,1024]{1,0:T(8,128)}) async-done(((f32[512,1024]{1,0:T(8,128)}, f32[512,1024]{1,0:T(8,128)}), (f32[512,1024]{1,0:T(8,128)}, f32[512,1024]{1,0:T(8,128)})) %all-reduce.7.cloned.1.call-update) | async-done | bytes 4194320 | tf_op jit(solution)/shard_map/psum | solution.py:15
  589.7 3.2 convolution_subtract_fusion.1
  594.9 3.5 convolution_subtract_fusion
  600.5 3.2 fusion.9
  605.0 4.5 fusion.5
  (131 shorter events, 88.3 us)
Async XLA Ops:
  7.2 252.0 %all-reduce.5.cloned.1.call-start = ((), (), s32[]{:S(2)}) async-start(), calls=%async_computation | async-start | bytes 2097152 | tf_op jit(solution)/shard_map/psum | solution.py:15
  22.6 1.0 copy-start.9
  35.3 0.6 copy-start.13
  110.2 61.0 %copy-start = (f32[512,512]{1,0:T(8,128)}, f32[512,512]{1,0:T(8,128)S(1)}, u32[]{:S(2)}) copy-start(f32[512,512]{1,0:T(8,128)S(1)} %get-tuple-element.57) | copy-start | bytes 3145732
  127.3 0.7 copy-start.15
  168.1 3.5 copy-start.1
  176.4 1.8 copy-start.7
  177.9 411.8 %all-reduce.7.cloned.1.call-start = ((), (), s32[]{:S(2)}) async-start(), calls=%async_computation.1 | async-start | bytes 8388608 | tf_op jit(solution)/shard_map/psum | solution.py:15
  259.1 3.6 copy-start.6
  270.1 1.0 copy-start.8
  282.8 0.6 copy-start.12
  382.3 0.7 copy-start.14
  423.4 3.5 copy-start.2
  589.7 3.3 copy-start.5
  589.7 3.3 copy-start.10
  593.0 1.9 copy-start.4
  603.8 1.2 copy-start.11
  605.0 4.5 copy-start.3
Sparse Core Ops, SparseCore 0:
  178.1 81.0 all-reduce.4
  433.7 155.9 all-reduce.6
where the time goes:
time: 627 us; the launch traced here: 617 us
  other arithmetic  258 us (41%)
  waiting for transfers between devices  236 us (38%)
  matrix products  56.9 us (9%)
  local copies, waits for them, and re-layouts  44.3 us (7%)
  between operations  21.3 us (3%)
    psum x2, waiting for transfers between devices, from_root(): return lax.psum(kept, axis)  236 us
    another operation x29, other arithmetic, factor_tile(): lower_tile = jnp.linalg.cholesky(square)  162 us
    another operation x5, other arithmetic, factor_tile(): lax.linalg.triangular_solve(lower_tile, identity_tile, left_side=True, lo...  83.9 us
    dot_general x8, matrix products, times_trans(): return lax.dot_general(left, right, CONTRACT, precision=HIGHEST)  25 us
    another operation x27, local copies, waits for them, and re-layouts, factor_tile(): lax.linalg.triangular_solve(lower_tile, identity_tile, left_side=True, lo...  23.5 us
    another operation x14, matrix products, factor_tile(): lax.linalg.triangular_solve(lower_tile, identity_tile, left_side=True, lo...  17.2 us
    another operation x12, matrix products, factor_tile(): lower_tile = jnp.linalg.cholesky(square)  14.7 us
  transfers between devices with their start and end apart: 2, of which 2 were waited for; matrix products, arithmetic and copies ran while one was open for 0% of the time, Pallas kernels for 0%

commit v1 on v0

v1 whole, which is shorter than its diff:
```python
import functools

import jax
import jax.numpy as jnp
from jax import lax
from jax.experimental import pallas as pl
from jax.experimental.pallas import tpu as pltpu
from jax.sharding import PartitionSpec as P

P_SIZE = 2
HIGHEST = lax.Precision.HIGHEST
CONTRACT = (((1,), (1,)), ((), ()))
LEAF = 128
GROUP = 8
WIDE = 256
MESH = pl.DeviceIdType.MESH


def times_trans(left, right):
    return lax.dot_general(left, right, CONTRACT, precision=HIGHEST, preferred_element_type=jnp.float32)


def spread_kernel(n_rows, n_cols, panel, first, second, row_send, row_recv, col_send, col_recv):
    r = lax.axis_index("rows")
    c = lax.axis_index("cols")
    width = panel.shape[0]
    share = width // n_cols
    pieces = []
    for half in range(2):
        pieces.append((0, half * (share // 2), share // 2))
    for quarter in range(4):
        pieces.append((1, quarter * (share // 4), share // 4))

    barrier = pltpu.get_barrier_semaphore()
    for step in range(1, n_cols):
        other = lax.rem(c + step, n_cols)
        pl.semaphore_signal(barrier, inc=1, device_id=(r, other), device_id_type=MESH)

    @pl.when(r < 2)
    def _():
        pl.semaphore_signal(barrier, inc=1, device_id=(1 - r, c), device_id_type=MESH)

    @pl.when(r >= 2)
    def _():
        pl.semaphore_signal(barrier, inc=1, device_id=(r - 2, c), device_id_type=MESH)

    @pl.when(r + 2 < n_rows)
    def _():
        pl.semaphore_signal(barrier, inc=1, device_id=(r + 2, c), device_id_type=MESH)

    pl.semaphore_wait(barrier, n_cols + (r + 2 < n_rows).astype(jnp.int32))

    def window(ref, piece, owner):
        which, start, size = pieces[piece]
        return ref.at[pl.ds(pl.multiple_of(owner * share + start, 8), size), :]

    def to_row(piece, slot, dest, own):
        which, start, size = pieces[piece]
        dst = window((first, second)[which], piece, c)
        if own:
            src = panel.at[pl.ds(pl.multiple_of(c * share + start, 8), size), pl.ds(0, dst.shape[1])]
        else:
            src = dst
        return pltpu.make_async_remote_copy(
            src_ref=src, dst_ref=dst, send_sem=row_send.at[piece, slot], recv_sem=row_recv.at[piece],
            device_id=(dest, c), device_id_type=MESH)

    def to_col(piece, step):
        ref = (first, second)[pieces[piece][0]]
        return pltpu.make_async_remote_copy(
            src_ref=window(ref, piece, c), dst_ref=window(ref, piece, c),
            send_sem=col_send.at[piece, step - 1], recv_sem=col_recv.at[piece, step - 1],
            device_id=(r, lax.rem(c + step, n_cols)), device_id_type=MESH)

    for piece in range(len(pieces)):
        which = pieces[piece][0]

        @pl.when(r == which)
        def _():
            to_row(piece, 0, 1 - which, True).start()
            if which + 2 < n_rows:
                to_row(piece, 1, which + 2, True).start()

    @pl.when(r == 0)
    def _():
        first[...] = panel[:, : first.shape[1]]

    @pl.when(r == 1)
    def _():
        second[...] = panel[...]

    for piece in range(len(pieces)):
        which = pieces[piece][0]

        @pl.when(r != which)
        def _():
            to_row(piece, 0, r, False).wait_recv()

            @pl.when(r + 2 < n_rows)
            def _():
                to_row(piece, 0, r + 2, False).start()

            for step in range(1, n_cols):
                to_col(piece, step).start()

    for piece in range(len(pieces)):
        which = pieces[piece][0]

        @pl.when(r != which)
        def _():
            for step in range(1, n_cols):
                to_col(piece, step).wait_recv()
            for step in range(1, n_cols):
                to_col(piece, step).wait_send()

            @pl.when(r + 2 < n_rows)
            def _():
                to_row(piece, 0, r + 2, False).wait_send()

        @pl.when(r == which)
        def _():
            to_row(piece, 0, 1 - which, True).wait_send()
            if which + 2 < n_rows:
                to_row(piece, 1, which + 2, True).wait_send()


def spread(panel, n_rows, n_cols):
    width = panel.shape[0]
    n_pieces = 6
    return pl.pallas_call(
        functools.partial(spread_kernel, n_rows, n_cols),
        out_shape=(
            jax.ShapeDtypeStruct((width, width), jnp.float32),
            jax.ShapeDtypeStruct((width, P_SIZE * width), jnp.float32),
        ),
        in_specs=[pl.BlockSpec(memory_space=pltpu.VMEM)],
        out_specs=(pl.BlockSpec(memory_space=pltpu.VMEM),) * 2,
        scratch_shapes=[
            pltpu.SemaphoreType.DMA((n_pieces, 2)),
            pltpu.SemaphoreType.DMA((n_pieces,)),
            pltpu.SemaphoreType.DMA((n_pieces, n_cols - 1)),
            pltpu.SemaphoreType.DMA((n_pieces, n_cols - 1)),
        ],
        compiler_params=pltpu.CompilerParams(
            collective_id=0, has_side_effects=True, vmem_limit_bytes=24 << 20),
        name="spread",
    )(panel)


def split3(value):
    high = value.astype(jnp.bfloat16).astype(jnp.float32)
    rest = value - high
    mid = rest.astype(jnp.bfloat16).astype(jnp.float32)
    return high, mid, rest - mid


def factor_leaf(aug, upper, inverse):
    lanes = lax.broadcasted_iota(jnp.int32, (GROUP, LEAF), 1)
    subs = lax.broadcasted_iota(jnp.int32, (GROUP, LEAF), 0)
    for g in range(LEAF // GROUP):
        base = g * GROUP
        left = aug[base : base + GROUP, :LEAF]
        right = aug[base : base + GROUP, LEAF:]
        cols = [
            jnp.broadcast_to(left[:, base + j : base + j + 1], (GROUP, LEAF)) for j in range(GROUP)
        ]
        scale = jnp.zeros((GROUP, LEAF), jnp.float32)
        for k in range(GROUP):
            pivot = jnp.broadcast_to(cols[k][k : k + 1, :], (GROUP, LEAF))
            root = lax.rsqrt(pivot)
            scale = jnp.where(subs == k, root, scale)
            if k + 1 < GROUP:
                mult = jnp.where(subs > k, cols[k] * (root * root), 0.0)
                for j in range(k + 1, GROUP):
                    cols[j] = cols[j] - mult * jnp.broadcast_to(cols[j][k : k + 1, :], (GROUP, LEAF))
                left = left - mult * jnp.broadcast_to(left[k : k + 1, :], (GROUP, LEAF))
                right = right - mult * jnp.broadcast_to(right[k : k + 1, :], (GROUP, LEAF))
        row_of = lanes - base
        left = jnp.where(row_of >= subs, left * scale, 0.0)
        right = right * scale
        upper[base : base + GROUP, :] = left
        inverse[base : base + GROUP, :] = right
        if base + GROUP < LEAF:
            lh, lm, ll = split3(left)
            rh, rm, rl = split3(right)
            keep = lanes >= base + GROUP
            a = [jnp.where(keep, v, 0.0) for v in (lh, lm, ll)]
            lhs = jnp.concatenate([a[0], a[0], a[1], a[0], a[1], a[2]], axis=0)
            rl_ = jnp.concatenate([lh, lm, lh, ll, lm, lh], axis=0)
            rr_ = jnp.concatenate([rh, rm, rh, rl, rm, rh], axis=0)
            rhs = jnp.concatenate([rl_, rr_], axis=1)
            update = lax.dot_general(
                lhs, rhs, (((0,), (0,)), ((), ())), preferred_element_type=jnp.float32)
            aug[base + GROUP :, :] = aug[base + GROUP :, :] - update[base + GROUP :, :]


def factor_kernel(first, second, lower, inverses, aug, upper, leaf_inv):
    width = first.shape[0]
    total = lower.shape[0]
    n_leaf = total // LEAF
    per = width // LEAF
    rows = lax.broadcasted_iota(jnp.int32, (LEAF, LEAF), 0)
    lanes = lax.broadcasted_iota(jnp.int32, (LEAF, LEAF), 1)
    lower[:width, :width] = first[...]
    lower[:width, width:] = jnp.zeros((width, total - width), jnp.float32)
    lower[width:, :] = second[...]
    for b in range(n_leaf - 1):
        lower[b * LEAF : (b + 1) * LEAF, (b + 1) * LEAF :] = jnp.zeros(
            (LEAF, total - (b + 1) * LEAF), jnp.float32)
    inverses[...] = jnp.zeros(inverses.shape, jnp.float32)

    def step(k, carry):
        at = pl.ds(pl.multiple_of(k * LEAF, LEAF), LEAF)
        block = lower[at, at]
        aug[:, :LEAF] = jnp.where(rows >= lanes, block, block.T)
        aug[:, LEAF:] = jnp.where(rows == lanes, 1.0, 0.0)
        factor_leaf(aug, upper, leaf_inv)
        lower[at, at] = upper[...].T
        for b in range(n_leaf):

            @pl.when(k == b)
            def _():
                lo, hi = b * LEAF, (b + 1) * LEAF
                wide = b * LEAF // WIDE
                off = lo - wide * WIDE
                inv = leaf_inv[...]
                inverses[wide, off : off + LEAF, off : off + LEAF] = inv
                if off:
                    before = inverses[wide, :LEAF, :LEAF]
                    cross = lower[lo:hi, lo - LEAF : lo]
                    part = lax.dot_general(
                        cross, before, (((1,), (0,)), ((), ())), precision=HIGHEST,
                        preferred_element_type=jnp.float32)
                    inverses[wide, LEAF:, :LEAF] = -lax.dot_general(
                        inv, part, (((1,), (0,)), ((), ())), precision=HIGHEST,
                        preferred_element_type=jnp.float32)
                if hi < total:
                    lower[hi:, lo:hi] = times_trans(lower[hi:, lo:hi], inv)
                    nxt = hi + LEAF
                    lower[hi:, hi:nxt] = lower[hi:, hi:nxt] - times_trans(
                        lower[hi:, :hi], lower[hi:nxt, :hi])

        return carry

    lax.fori_loop(0, n_leaf, step, 0)


def factor_head(first, second):
    width = first.shape[0]
    total = P_SIZE * width
    return pl.pallas_call(
        factor_kernel,
        out_shape=(
            jax.ShapeDtypeStruct((total, total), jnp.float32),
            jax.ShapeDtypeStruct((total // WIDE, WIDE, WIDE), jnp.float32),
        ),
        in_specs=[pl.BlockSpec(memory_space=pltpu.VMEM)] * 2,
        out_specs=(pl.BlockSpec(memory_space=pltpu.VMEM),) * 2,
        scratch_shapes=[
            pltpu.VMEM((LEAF, 2 * LEAF), jnp.float32),
            pltpu.VMEM((LEAF, LEAF), jnp.float32),
            pltpu.VMEM((LEAF, LEAF), jnp.float32),
        ],
        compiler_params=pltpu.CompilerParams(vmem_limit_bytes=32 << 20),
        cost_estimate=pl.CostEstimate(flops=10**10, bytes_accessed=10**7, transcendentals=0),
        name="factor_head",
    )(first, second)


def solve_into(out, lower, inverses):
    for wide in range(lower.shape[0] // WIDE):
        lo, hi = wide * WIDE, (wide + 1) * WIDE
        now = out[:, lo:hi]
        if wide:
            now = now - times_trans(out[:, :lo], lower[lo:hi, :lo])
        out[:, lo:hi] = times_trans(now, inverses[wide])


def own_kernel(live, panel, lower, inverses, factor):
    r = lax.axis_index("rows")
    width = panel.shape[0]

    @pl.when(r < P_SIZE)
    def _():
        factor[...] = lower[pl.ds(pl.multiple_of(lax.rem(r, P_SIZE) * width, width), width), :]

    @pl.when(r >= P_SIZE)
    def _():
        factor[...] = panel[...] * live[0]
        solve_into(factor, lower, inverses)


def own_rows(live, panel, lower, inverses):
    return pl.pallas_call(
        own_kernel,
        out_shape=jax.ShapeDtypeStruct(panel.shape, jnp.float32),
        in_specs=[pl.BlockSpec(memory_space=pltpu.SMEM)] + [pl.BlockSpec(memory_space=pltpu.VMEM)] * 3,
        out_specs=pl.BlockSpec(memory_space=pltpu.VMEM),
        compiler_params=pltpu.CompilerParams(vmem_limit_bytes=32 << 20),
        cost_estimate=pl.CostEstimate(flops=10**9, bytes_accessed=10**7, transcendentals=0),
        name="own_rows",
    )(live, panel, lower, inverses)


def update_kernel(target, lower, inverses, factor, window, updated, row):
    row[...] = target[...]
    solve_into(row, lower, inverses)
    updated[...] = window[...] - times_trans(factor[...], row[...])


def update_window(target, lower, inverses, factor, window):
    return pl.pallas_call(
        update_kernel,
        out_shape=jax.ShapeDtypeStruct(window.shape, jnp.float32),
        in_specs=[pl.BlockSpec(memory_space=pltpu.VMEM)] * 5,
        out_specs=pl.BlockSpec(memory_space=pltpu.VMEM),
        scratch_shapes=[pltpu.VMEM(target.shape, jnp.float32)],
        compiler_params=pltpu.CompilerParams(vmem_limit_bytes=40 << 20),
        cost_estimate=pl.CostEstimate(flops=10**9, bytes_accessed=10**7, transcendentals=0),
        name="update_window",
    )(target, lower, inverses, factor, window)


def shards(n_rows, n_cols, panel, window_block, row_live, window_rows):
    device_row = lax.axis_index("rows")
    device_col = lax.axis_index("cols")
    live = jnp.where(device_row < P_SIZE, 1, row_live[device_row]).astype(jnp.float32)
    first, second = spread(panel, n_rows, n_cols)
    first, second, panel = lax.optimization_barrier((first, second, panel))
    target = window_rows[device_col]
    kept = jnp.where(device_row == target, panel * live, 0)
    target_raw = lax.psum(kept, "rows")
    lower, inverses = factor_head(first, second)
    factor = own_rows(live[None], panel, lower, inverses)
    updated = update_window(target_raw, lower, inverses, factor, window_block)
    return (factor, updated)


def solution(mesh):
    in_specs = (P("rows", None), P("rows", "cols"), P(), P())
    out_specs = (P("rows", None), P("rows", "cols"))
    body = functools.partial(shards, mesh.shape["rows"], mesh.shape["cols"])
    return jax.shard_map(body, mesh=mesh, in_specs=in_specs, out_specs=out_specs, check_vma=False)
```

time: 627 us -> 203 us (0.32); the launches traced: 617 us -> 203 us
  other arithmetic: 258 us -> 1.71 us
  waiting for transfers between devices: 236 us -> 67.6 us
  Pallas kernels: 0 us -> 105 us
  matrix products: 56.9 us -> 0 us
  local copies, waits for them, and re-layouts: 44.3 us -> 13.6 us
    another operation x34 -> x0, other arithmetic: 246 us -> none  [the longest x29 162 us: factor_tile(): lower_tile = jnp.linalg.cholesky(square)]
    psum x2 -> x1, waiting for transfers between devices: 236 us -> 67.6 us  [shards(): target_raw = lax.psum(kept, 'rows')]
    pallas_call x0 -> x4, Pallas kernels: none -> 105 us  [the longest x1 60 us: factor_head(): pl.pallas_call(factor_kernel, out_shape=(jax.ShapeDtypeStruct((total, tot...]
    another operation x26 -> x0, matrix products: 31.9 us -> none  [the longest x14 17.2 us: factor_tile(): lax.linalg.triangular_solve(lower_tile, identity_tile, left_side=True, lo...]
    another operation x39 -> x0, local copies, waits for them, and re-layouts: 28.3 us -> none  [the longest x27 23.5 us: factor_tile(): lax.linalg.triangular_solve(lower_tile, identity_tile, left_side=True, lo...]
    dot_general x8 -> x0, matrix products: 25 us -> none  [times_trans(): return lax.dot_general(left, right, CONTRACT, precision=HIGHEST)]
  transfers between devices with their start and end apart: 2 -> 1, of which waited for: 2 -> 1; matrix products, arithmetic and copies ran while one was open for 0% -> 0% of each run, Pallas kernels for 0% -> 30%
where the time goes in v1:
time: 203 us
  Pallas kernels  105 us (52%)
  waiting for transfers between devices  67.6 us (33%)
  between operations  15.4 us (8%)
  local copies, waits for them, and re-layouts  13.6 us (7%)
    psum x1, waiting for transfers between devices, shards(): target_raw = lax.psum(kept, 'rows')  67.6 us
    pallas_call x1, Pallas kernels, factor_head(): pl.pallas_call(factor_kernel, out_shape=(jax.ShapeDtypeStruct((total, tot...  60 us
    pallas_call x1, Pallas kernels, spread(): pl.pallas_call(functools.partial(spread_kernel, n_rows, n_cols), out_shap...  31.1 us
    pallas_call x1, Pallas kernels, update_window(): pl.pallas_call(update_kernel, out_shape=jax.ShapeDtypeStruct(window.shape...  11.8 us
    unnamed x18, local copies, waits for them, and re-layouts  11.1 us
  transfers between devices with their start and end apart: 1, of which 1 were waited for; matrix products, arithmetic and copies ran while one was open for 0% of the time, Pallas kernels for 30%

profile of v1, /device:TPU:0, one launch (start us, length us, event | category | flops | bytes accessed | tf_op | source)
XLA Modules:
  0.0 202.9 jit_solution(6289136787077598201)
XLA Ops:
  7.2 0.0 all-reduce.2.cloned.1.call-start
  7.2 1.2 dynamic_slice.7
  9.1 1.2 dynamic_slice.6
  11.0 0.0 copy-start
  11.0 1.6 copy-done
  12.6 31.1 %spread.1 = (f32[512,512]{1,0:T(8,128)S(1)}, f32[512,1024]{1,0:T(8,128)S(1)}) custom-call(f32[512,1024]{1,0:T(8,128)S(1)} %copy-done), custom_call_target="tpu_custom_call" | custom-call | tf_op jit(solution)/shard_map/spread/pallas_call | solution.py:130
  43.7 0.0 copy-start.7
  43.7 1.0 copy-done.7
  44.7 1.7 multiply_select_fusion
  46.4 0.0 all-reduce.2.cloned.1.call-update
  46.4 0.0 copy-start.8
  46.4 1.2 copy-done.8
  47.6 0.0 copy-start.1
  47.6 60.0 %factor_head.1 = (f32[1024,1024]{1,0:T(8,128)S(1)}, f32[4,256,256]{2,1,0:T(8,128)S(1)}) custom-call(f32[512,512]{1,0:T(8,128)S(1)} %copy-done.8, f32[512,1024]{1,0:T(8,128)S(1)} %get-tuple-element.13.second), custom_call_target="tpu_custom_call" | custom-call | flops 10000000000 | bytes 10000000 | tf_op jit(solution)/shard_map/factor_head/pallas_call | solution.py:251
  107.7 0.0 copy-done.1
  107.7 0.0 copy-start.6
  107.7 1.7 own_rows.1.factor
  109.4 0.0 copy-start.2
  109.4 2.0 copy-done.2
  111.3 67.6 %all-reduce.2.cloned.1.call-done.target = f32[512,1024]{1,0:T(8,128)} async-done(((f32[512,1024]{1,0:T(8,128)}), f32[512,1024]{1,0:T(8,128)}) %all-reduce.2.cloned.1.call-update) | async-done | bytes 2097168 | tf_op jit(solution)/shard_map/psum | solution.py:332
  178.9 0.0 copy-done.6
  178.9 0.0 copy-start.3
  178.9 2.2 %copy-done.3 = f32[1024,1024]{1,0:T(8,128)S(1)} copy-done((f32[1024,1024]{1,0:T(8,128)S(1)}, f32[1024,1024]{1,0:T(8,128)}, u32[]{:S(2)}) %copy-start.3) | copy-done | bytes 4194328
  181.1 0.0 copy-start.4
  181.1 1.6 copy-done.4
  182.7 0.0 copy-start.5
  182.7 1.6 copy-done.5
  184.3 11.8 %update_window.1 = f32[512,512]{1,0:T(8,128)} custom-call(f32[512,1024]{1,0:T(8,128)S(1)} %copy-done.5, f32[1024,1024]{1,0:T(8,128)S(1)} %copy-done.3, f32[4,256,256]{2,1,0:T(8,128)S(1)} %get-tuple-element.15.inverses, f32[512,1024]{1,0:T(8,128)S(1)} %copy-done.4, f32[512,512]{1,0:T(8,128)S(1)} %copy-done.6), custom_call_target="tpu_custom_call" | custom-call | flops 1000000000 | bytes 10000000 | tf_op jit(solution)/shard_map/update_window/pallas_call | solution.py:312
Async XLA Ops:
  7.2 171.8 %all-reduce.2.cloned.1.call-start = ((), (), s32[]{:S(2)}) async-start(), calls=%async_computation | async-start | bytes 4194304 | tf_op jit(solution)/shard_map/psum | solution.py:332
  11.0 1.6 copy-start
  43.7 1.0 copy-start.7
  46.4 1.2 copy-start.8
  47.6 60.1 %copy-start.1 = (f32[512,1024]{1,0:T(8,128)S(1)}, f32[512,1024]{1,0:T(8,128)}, u32[]{:S(2)}) copy-start(f32[512,1024]{1,0:T(8,128)} %panel.2) | copy-start | bytes 6291460
  107.7 71.2 %copy-start.6 = (f32[512,512]{1,0:T(8,128)S(1)}, f32[512,512]{1,0:T(8,128)}, u32[]{:S(2)}) copy-start(f32[512,512]{1,0:T(8,128)} %window.1) | copy-start | bytes 3145732
  109.4 2.0 copy-start.2
  178.9 2.2 %copy-start.3 = (f32[1024,1024]{1,0:T(8,128)S(1)}, f32[1024,1024]{1,0:T(8,128)}, u32[]{:S(2)}) copy-start(f32[1024,1024]{1,0:T(8,128)} %copy-done.2) | copy-start | bytes 12582916
  181.1 1.6 copy-start.4
  182.7 1.6 copy-start.5
Sparse Core Ops, SparseCore 0:
  46.5 132.3 all-reduce.1

commit v2 on v1

--- a/solution.py
+++ b/solution.py
@@ -10,30 +10,48 @@
 P_SIZE = 2
 HIGHEST = lax.Precision.HIGHEST
 CONTRACT = (((1,), (1,)), ((), ()))
+PLAIN = (((1,), (0,)), ((), ()))
 LEAF = 128
 GROUP = 8
 WIDE = 256
 MESH = pl.DeviceIdType.MESH
 
 
+def halves(value):
+    high = value.astype(jnp.bfloat16)
+    return high, (value - high.astype(jnp.float32)).astype(jnp.bfloat16)
+
+
+def product(left, right, contract):
+    lh, ll = halves(left)
+    rh, rl = halves(right)
+
+    def dot(a, b):
+        return lax.dot_general(a, b, contract, preferred_element_type=jnp.float32)
+
+    return dot(lh, rh) + (dot(lh, rl) + dot(ll, rh))
+
+
 def times_trans(left, right):
-    return lax.dot_general(left, right, CONTRACT, precision=HIGHEST, preferred_element_type=jnp.float32)
-
-
-def spread_kernel(n_rows, n_cols, panel, first, second, row_send, row_recv, col_send, col_recv):
+    return product(left, right, CONTRACT)
+
+
+def times(left, right):
+    return product(left, right, PLAIN)
+
+
+def spread_kernel(n_rows, panel, first, second, row_send, row_recv, far_send, far_recv, near_send, near_recv):
     r = lax.axis_index("rows")
     c = lax.axis_index("cols")
+    far = lax.rem(c + 2, 4)
+    near = c + 1 - 2 * lax.rem(c, 2)
     width = panel.shape[0]
-    share = width // n_cols
-    pieces = []
-    for half in range(2):
-        pieces.append((0, half * (share // 2), share // 2))
-    for quarter in range(4):
-        pieces.append((1, quarter * (share // 4), share // 4))
+    n_blocks = width // LEAF
+    share = LEAF // 4
+    pieces = [(which, b) for which in range(2) for b in range(n_blocks)]
 
     barrier = pltpu.get_barrier_semaphore()
-    for step in range(1, n_cols):
-        other = lax.rem(c + step, n_cols)
+    for other in (far, near):
         pl.semaphore_signal(barrier, inc=1, device_id=(r, other), device_id_type=MESH)
 
     @pl.when(r < 2)
@@ -48,29 +66,34 @@
     def _():
         pl.semaphore_signal(barrier, inc=1, device_id=(r + 2, c), device_id_type=MESH)
 
-    pl.semaphore_wait(barrier, n_cols + (r + 2 < n_rows).astype(jnp.int32))
+    pl.semaphore_wait(barrier, 3 + (r + 2 < n_rows).astype(jnp.int32))
 
     def window(ref, piece, owner):
-        which, start, size = pieces[piece]
-        return ref.at[pl.ds(pl.multiple_of(owner * share + start, 8), size), :]
+        which, b = pieces[piece]
+        start = pl.multiple_of(b * LEAF + owner * share, 8)
+        return ref.at[pl.ds(start, share), pl.ds(0, which * width + (b + 1) * LEAF)]
+
+    def landing(piece, owner):
+        return window((first, second)[pieces[piece][0]], piece, owner)
 
     def to_row(piece, slot, dest, own):
-        which, start, size = pieces[piece]
-        dst = window((first, second)[which], piece, c)
-        if own:
-            src = panel.at[pl.ds(pl.multiple_of(c * share + start, 8), size), pl.ds(0, dst.shape[1])]
-        else:
-            src = dst
         return pltpu.make_async_remote_copy(
-            src_ref=src, dst_ref=dst, send_sem=row_send.at[piece, slot], recv_sem=row_recv.at[piece],
+            src_ref=window(panel, piece, c) if own else landing(piece, c), dst_ref=landing(piece, c),
+            send_sem=row_send.at[piece, slot], recv_sem=row_recv.at[piece],
             device_id=(dest, c), device_id_type=MESH)
 
-    def to_col(piece, step):
-        ref = (first, second)[pieces[piece][0]]
+    def to_far(piece):
         return pltpu.make_async_remote_copy(
-            src_ref=window(ref, piece, c), dst_ref=window(ref, piece, c),
-            send_sem=col_send.at[piece, step - 1], recv_sem=col_recv.at[piece, step - 1],
-            device_id=(r, lax.rem(c + step, n_cols)), device_id_type=MESH)
+            src_ref=landing(piece, c), dst_ref=landing(piece, c),
+            send_sem=far_send.at[piece], recv_sem=far_recv.at[piece],
+            device_id=(r, far), device_id_type=MESH)
+
+    def to_near(piece, slot):
+        owner = (c, far)[slot]
+        return pltpu.make_async_remote_copy(
+            src_ref=landing(piece, owner), dst_ref=landing(piece, owner),
+            send_sem=near_send.at[piece, slot], recv_sem=near_recv.at[piece, slot],
+            device_id=(r, near), device_id_type=MESH)
 
     for piece in range(len(pieces)):
         which = pieces[piece][0]
@@ -83,35 +106,43 @@
 
     @pl.when(r == 0)
     def _():
-        first[...] = panel[:, : first.shape[1]]
+        first[...] = panel[:, :width]
 
     @pl.when(r == 1)
     def _():
         second[...] = panel[...]
+
+    for piece in range(len(pieces) + 1):
+        if piece < len(pieces):
+
+            @pl.when(r != pieces[piece][0])
+            def _():
+                to_row(piece, 0, r, False).wait_recv()
+
+                @pl.when(r + 2 < n_rows)
+                def _():
+                    to_row(piece, 0, r + 2, False).start()
+
+                to_far(piece).start()
+                to_near(piece, 0).start()
+
+        if piece > 0:
+
+            @pl.when(r != pieces[piece - 1][0])
+            def _():
+                to_far(piece - 1).wait_recv()
+                to_near(piece - 1, 1).start()
 
     for piece in range(len(pieces)):
         which = pieces[piece][0]
 
         @pl.when(r != which)
         def _():
-            to_row(piece, 0, r, False).wait_recv()
-
-            @pl.when(r + 2 < n_rows)
-            def _():
-                to_row(piece, 0, r + 2, False).start()
-
-            for step in range(1, n_cols):
-                to_col(piece, step).start()
-
-    for piece in range(len(pieces)):
-        which = pieces[piece][0]
-
-        @pl.when(r != which)
-        def _():
-            for step in range(1, n_cols):
-                to_col(piece, step).wait_recv()
-            for step in range(1, n_cols):
-                to_col(piece, step).wait_send()
+            for slot in range(2):
+                to_near(piece, slot).wait_recv()
+            for slot in range(2):
+                to_near(piece, slot).wait_send()
+            to_far(piece).wait_send()
 
             @pl.when(r + 2 < n_rows)
             def _():
@@ -125,10 +156,12 @@
 
 
 def spread(panel, n_rows, n_cols):
+    if n_cols != 4 or n_rows < 2:
+        raise ValueError("unsupported mesh")
     width = panel.shape[0]
-    n_pieces = 6
+    n_pieces = 2 * (width // LEAF)
     return pl.pallas_call(
-        functools.partial(spread_kernel, n_rows, n_cols),
+        functools.partial(spread_kernel, n_rows),
         out_shape=(
             jax.ShapeDtypeStruct((width, width), jnp.float32),
             jax.ShapeDtypeStruct((width, P_SIZE * width), jnp.float32),
@@ -138,11 +171,14 @@
         scratch_shapes=[
             pltpu.SemaphoreType.DMA((n_pieces, 2)),
             pltpu.SemaphoreType.DMA((n_pieces,)),
-            pltpu.SemaphoreType.DMA((n_pieces, n_cols - 1)),
-            pltpu.SemaphoreType.DMA((n_pieces, n_cols - 1)),
+            pltpu.SemaphoreType.DMA((n_pieces,)),
+            pltpu.SemaphoreType.DMA((n_pieces,)),
+            pltpu.SemaphoreType.DMA((n_pieces, 2)),
+            pltpu.SemaphoreType.DMA((n_pieces, 2)),
         ],
         compiler_params=pltpu.CompilerParams(
             collective_id=0, has_side_effects=True, vmem_limit_bytes=24 << 20),
+        cost_estimate=pl.CostEstimate(flops=10**9, bytes_accessed=10**7, transcendentals=0),
         name="spread",
     )(panel)
 
@@ -194,7 +230,7 @@
             aug[base + GROUP :, :] = aug[base + GROUP :, :] - update[base + GROUP :, :]
 
 
-def factor_kernel(first, second, lower, inverses, aug, upper, leaf_inv):
+def factor_kernel(live, first, second, panel, factor, solved, lower, inverses, aug, upper, leaf_inv):
     width = first.shape[0]
     total = lower.shape[0]
     n_leaf = total // LEAF
@@ -244,95 +280,79 @@
 
     lax.fori_loop(0, n_leaf, step, 0)
 
-
-def factor_head(first, second):
+    r = lax.axis_index("rows")
+    n_wide = total // WIDE
+
+    @pl.when(r < P_SIZE)
+    def _():
+        factor[...] = lower[pl.ds(pl.multiple_of(lax.rem(r, P_SIZE) * width, width), width), :]
+
+    @pl.when(r >= P_SIZE)
+    def _():
+        factor[...] = panel[...] * live[0]
+        for wide in range(n_wide):
+            lo, hi = wide * WIDE, (wide + 1) * WIDE
+            now = factor[:, lo:hi]
+            if wide:
+                now = now - times_trans(factor[:, :lo], lower[lo:hi, :lo])
+            factor[:, lo:hi] = times_trans(now, inverses[wide])
+
+    for wide in reversed(range(n_wide)):
+        lo, hi = wide * WIDE, (wide + 1) * WIDE
+        now = factor[:, lo:hi]
+        if hi < total:
+            now = now - times(solved[:, hi:], lower[hi:, lo:hi])
+        solved[:, lo:hi] = times(now, inverses[wide])
+
+
+def factor_rows(live, first, second, panel):
     width = first.shape[0]
     total = P_SIZE * width
     return pl.pallas_call(
         factor_kernel,
-        out_shape=(
-            jax.ShapeDtypeStruct((total, total), jnp.float32),
-            jax.ShapeDtypeStruct((total // WIDE, WIDE, WIDE), jnp.float32),
-        ),
-        in_specs=[pl.BlockSpec(memory_space=pltpu.VMEM)] * 2,
+        out_shape=(jax.ShapeDtypeStruct(panel.shape, jnp.float32),) * 2,
+        in_specs=[pl.BlockSpec(memory_space=pltpu.SMEM)] + [pl.BlockSpec(memory_space=pltpu.VMEM)] * 3,
         out_specs=(pl.BlockSpec(memory_space=pltpu.VMEM),) * 2,
         scratch_shapes=[
+            pltpu.VMEM((total, total), jnp.float32),
+            pltpu.VMEM((total // WIDE, WIDE, WIDE), jnp.float32),
             pltpu.VMEM((LEAF, 2 * LEAF), jnp.float32),
             pltpu.VMEM((LEAF, LEAF), jnp.float32),
             pltpu.VMEM((LEAF, LEAF), jnp.float32),
         ],
-        compiler_params=pltpu.CompilerParams(vmem_limit_bytes=32 << 20),
+        compiler_params=pltpu.CompilerParams(vmem_limit_bytes=40 << 20),
         cost_estimate=pl.CostEstimate(flops=10**10, bytes_accessed=10**7, transcendentals=0),
-        name="factor_head",
-    )(first, second)
-
-
-def solve_into(out, lower, inverses):
-    for wide in range(lower.shape[0] // WIDE):
-        lo, hi = wide * WIDE, (wide + 1) * WIDE
-        now = out[:, lo:hi]
-        if wide:
-            now = now - times_trans(out[:, :lo], lower[lo:hi, :lo])
-        out[:, lo:hi] = times_trans(now, inverses[wide])
-
-
-def own_kernel(live, panel, lower, inverses, factor):
-    r = lax.axis_index("rows")
-    width = panel.shape[0]
-
-    @pl.when(r < P_SIZE)
-    def _():
-        factor[...] = lower[pl.ds(pl.multiple_of(lax.rem(r, P_SIZE) * width, width), width), :]
-
-    @pl.when(r >= P_SIZE)
-    def _():
-        factor[...] = panel[...] * live[0]
-        solve_into(factor, lower, inverses)
-
-
-def own_rows(live, panel, lower, inverses):
-    return pl.pallas_call(
-        own_kernel,
-        out_shape=jax.ShapeDtypeStruct(panel.shape, jnp.float32),
-        in_specs=[pl.BlockSpec(memory_space=pltpu.SMEM)] + [pl.BlockSpec(memory_space=pltpu.VMEM)] * 3,
-        out_specs=pl.BlockSpec(memory_space=pltpu.VMEM),
-        compiler_params=pltpu.CompilerParams(vmem_limit_bytes=32 << 20),
-        cost_estimate=pl.CostEstimate(flops=10**9, bytes_accessed=10**7, transcendentals=0),
-        name="own_rows",
-    )(live, panel, lower, inverses)
-
-
-def update_kernel(target, lower, inverses, factor, window, updated, row):
-    row[...] = target[...]
-    solve_into(row, lower, inverses)
-    updated[...] = window[...] - times_trans(factor[...], row[...])
-
-
-def update_window(target, lower, inverses, factor, window):
+        name="factor_rows",
+    )(live, first, second, panel)
+
+
+def update_kernel(solved, target, window, updated):
+    updated[...] = window[...] - times_trans(solved[...], target[...])
+
+
+def update_window(solved, target, window):
     return pl.pallas_call(
         update_kernel,
         out_shape=jax.ShapeDtypeStruct(window.shape, jnp.float32),
-        in_specs=[pl.BlockSpec(memory_space=pltpu.VMEM)] * 5,
+        in_specs=[pl.BlockSpec(memory_space=pltpu.VMEM)] * 3,
         out_specs=pl.BlockSpec(memory_space=pltpu.VMEM),
-        scratch_shapes=[pltpu.VMEM(target.shape, jnp.float32)],
         compiler_params=pltpu.CompilerParams(vmem_limit_bytes=40 << 20),
         cost_estimate=pl.CostEstimate(flops=10**9, bytes_accessed=10**7, transcendentals=0),
         name="update_window",
-    )(target, lower, inverses, factor, window)
+    )(solved, target, window)
 
 
 def shards(n_rows, n_cols, panel, window_block, row_live, window_rows):
     device_row = lax.axis_index("rows")
     device_col = lax.axis_index("cols")
     live = jnp.where(device_row < P_SIZE, 1, row_live[device_row]).astype(jnp.float32)
-    first, second = spread(panel, n_rows, n_cols)
-    first, second, panel = lax.optimization_barrier((first, second, panel))
     target = window_rows[device_col]
     kept = jnp.where(device_row == target, panel * live, 0)
+    kept, panel = lax.optimization_barrier((kept, panel))
     target_raw = lax.psum(kept, "rows")
-    lower, inverses = factor_head(first, second)
-    factor = own_rows(live[None], panel, lower, inverses)
-    updated = update_window(target_raw, lower, inverses, factor, window_block)
+    first, second = spread(panel, n_rows, n_cols)
+    factor, solved = factor_rows(live[None], first, second, panel)
+    updated = update_window(solved, target_raw, window_block)
     return (factor, updated)
 
 

time: 203 us -> 152 us (0.75)
  the two profiles are of different devices: /device:TPU:0 before, /device:TPU:27 now
where the time goes in v2:
time: 152 us
  Pallas kernels  127 us (84%)
  between operations  15.4 us (10%)
  local copies, waits for them, and re-layouts  5.64 us (4%)
  other arithmetic  3.29 us (2%)
    pallas_call x1, Pallas kernels, factor_rows(): pl.pallas_call(factor_kernel, out_shape=(jax.ShapeDtypeStruct(panel.shape...  65.1 us
    pallas_call x1, Pallas kernels, spread(): pl.pallas_call(functools.partial(spread_kernel, n_rows), out_shape=(jax.S...  59.2 us
    select_n x1, other arithmetic, shards(): kept = jnp.where(device_row == target, panel * live, 0)  3.29 us
    unnamed x8, local copies, waits for them, and re-layouts  3.16 us
  transfers between devices with their start and end apart: 1, of which 0 were waited for; matrix products, arithmetic and copies ran while one was open for 0% of the time, Pallas kernels for 82%

profile of v2, /device:TPU:27, one launch (start us, length us, event | category | flops | bytes accessed | tf_op | source)
XLA Modules:
  0.0 151.6 jit_solution(12691895117395048294)
XLA Ops:
  7.2 0.0 all-reduce.2.cloned.1.call-start
  7.2 1.2 dynamic_slice.7
  9.1 1.2 dynamic_slice.6
  11.0 3.3 %multiply_select_fusion = f32[512,1024]{1,0:T(8,128)} fusion(f32[512,1024]{1,0:T(8,128)} %panel.1, f32[]{:T(128)} %convert_element_type.5, pred[]{:T(512)S(6)} %eq.3), kind=kLoop, calls=%fused_computation | loop fusion | flops 1048576 | bytes 4194309 | tf_op jit(solution)/shard_map/jit(_where)/select_n | solution.py:350
  14.3 0.0 copy-start.1
  14.3 0.0 all-reduce.2.cloned.1.call-update
  14.3 1.6 %copy-done.1 = f32[512,1024]{1,0:T(8,128)S(1)} copy-done((f32[512,1024]{1,0:T(8,128)S(1)}, f32[512,1024]{1,0:T(8,128)}, u32[]{:S(2)}) %copy-start.1) | copy-done | bytes 2097176
  15.9 0.0 copy-start.2
  15.9 59.2 %spread.1 = (f32[512,512]{1,0:T(8,128)S(1)}, f32[512,1024]{1,0:T(8,128)S(1)}) custom-call(f32[512,1024]{1,0:T(8,128)S(1)} %copy-done.1), custom_call_target="tpu_custom_call" | custom-call | flops 1000000000 | bytes 10000000 | tf_op jit(solution)/shard_map/spread/pallas_call | solution.py:163
  75.1 0.0 copy-done.2
  75.1 0.0 copy-start.3
  75.1 65.1 %factor_rows.1 = (f32[512,1024]{1,0:T(8,128)}, f32[512,1024]{1,0:T(8,128)S(1)}) custom-call(f32[1]{0:T(128)} %bitcast.1.live, f32[512,512]{1,0:T(8,128)S(1)} %get-tuple-element.9.first, f32[512,1024]{1,0:T(8,128)S(1)} %get-tuple-element.10.second, f32[512,1024]{1,0:T(8,128)S(1)} %copy-done.2), custom_call_target="tpu_custom_call" | custom-call | flops 10000000000 | bytes 10000000 | tf_op jit(solution)/shard_map/factor_rows/pallas_call | solution.py:311
  140.3 0.0 all-reduce.2.cloned.1.call-done.target
  140.3 0.0 copy-done.3
  140.3 0.0 copy-start
  140.3 1.6 %copy-done = f32[512,1024]{1,0:T(8,128)S(1)} copy-done((f32[512,1024]{1,0:T(8,128)S(1)}, f32[512,1024]{1,0:T(8,128)}, u32[]{:S(2)}) %copy-start) | copy-done | bytes 2097176
  141.9 2.8 %update_window.1 = f32[512,512]{1,0:T(8,128)} custom-call(f32[512,1024]{1,0:T(8,128)S(1)} %get-tuple-element.12.solved, f32[512,1024]{1,0:T(8,128)S(1)} %copy-done, f32[512,512]{1,0:T(8,128)S(1)} %copy-done.3), custom_call_target="tpu_custom_call" | custom-call | flops 1000000000 | bytes 10000000 | tf_op jit(solution)/shard_map/update_window/pallas_call | solution.py:334
Async XLA Ops:
  7.2 133.1 %all-reduce.2.cloned.1.call-start = ((), (), s32[]{:S(2)}) async-start(), calls=%async_computation | async-start | bytes 4194304 | tf_op jit(solution)/shard_map/psum | solution.py:352
  14.3 1.6 %copy-start.1 = (f32[512,1024]{1,0:T(8,128)S(1)}, f32[512,1024]{1,0:T(8,128)}, u32[]{:S(2)}) copy-start(f32[512,1024]{1,0:T(8,128)} %panel.1) | copy-start | bytes 6291460
  15.9 59.2 %copy-start.2 = (f32[512,1024]{1,0:T(8,128)S(1)}, f32[512,1024]{1,0:T(8,128)}, u32[]{:S(2)}) copy-start(f32[512,1024]{1,0:T(8,128)} %panel.1) | copy-start | bytes 6291460
  75.1 65.2 %copy-start.3 = (f32[512,512]{1,0:T(8,128)S(1)}, f32[512,512]{1,0:T(8,128)}, u32[]{:S(2)}) copy-start(f32[512,512]{1,0:T(8,128)} %window.1) | copy-start | bytes 3145732
  140.3 1.6 %copy-start = (f32[512,1024]{1,0:T(8,128)S(1)}, f32[512,1024]{1,0:T(8,128)}, u32[]{:S(2)}) copy-start(f32[512,1024]{1,0:T(8,128)} %all-reduce.2.cloned.1.call-done.target) | copy-start | bytes 6291460
Sparse Core Ops, SparseCore 0:
  14.4 112.4 all-reduce.1

commit v3 on v2

--- a/solution.py
+++ b/solution.py
@@ -12,7 +12,7 @@
 CONTRACT = (((1,), (1,)), ((), ()))
 PLAIN = (((1,), (0,)), ((), ()))
 LEAF = 128
-GROUP = 8
+GROUP = 16
 WIDE = 256
 MESH = pl.DeviceIdType.MESH
 

time: 152 us -> 142 us (0.934)
  the two profiles are of different devices: /device:TPU:27 before, /device:TPU:0 now
where the time goes in v3:
time: 142 us; the launch traced here: 141 us
  Pallas kernels  73.5 us (52%)
  waiting for transfers between devices  43.5 us (31%)
  between operations  15.4 us (11%)
  local copies, waits for them, and re-layouts  5.65 us (4%)
  other arithmetic  3.29 us (2%)
    pallas_call x1, Pallas kernels, factor_rows(): pl.pallas_call(factor_kernel, out_shape=(jax.ShapeDtypeStruct(panel.shape...  43.5 us
    psum x1, waiting for transfers between devices, shards(): target_raw = lax.psum(kept, 'rows')  43.5 us
    pallas_call x1, Pallas kernels, spread(): pl.pallas_call(functools.partial(spread_kernel, n_rows), out_shape=(jax.S...  27.2 us
    select_n x1, other arithmetic, shards(): kept = jnp.where(device_row == target, panel * live, 0)  3.29 us
    unnamed x8, local copies, waits for them, and re-layouts  3.17 us
  transfers between devices with their start and end apart: 1, of which 1 were waited for; matrix products, arithmetic and copies ran while one was open for 0% of the time, Pallas kernels for 50%

profile of v3, /device:TPU:0, one launch (start us, length us, event | category | flops | bytes accessed | tf_op | source)
XLA Modules:
  0.0 141.4 jit_solution(3059885506120330226)
XLA Ops:
  7.2 0.0 all-reduce.2.cloned.1.call-start
  7.2 1.2 dynamic_slice.7
  9.1 1.2 dynamic_slice.6
  11.0 3.3 %multiply_select_fusion = f32[512,1024]{1,0:T(8,128)} fusion(f32[512,1024]{1,0:T(8,128)} %panel.1, f32[]{:T(128)} %convert_element_type.5, pred[]{:T(512)S(6)} %eq.3), kind=kLoop, calls=%fused_computation | loop fusion | flops 1048576 | bytes 4194309 | tf_op jit(solution)/shard_map/jit(_where)/select_n | solution.py:350
  14.3 0.0 copy-start.1
  14.3 0.0 all-reduce.2.cloned.1.call-update
  14.3 1.6 %copy-done.1 = f32[512,1024]{1,0:T(8,128)S(1)} copy-done((f32[512,1024]{1,0:T(8,128)S(1)}, f32[512,1024]{1,0:T(8,128)}, u32[]{:S(2)}) %copy-start.1) | copy-done | bytes 2097176
  15.9 0.0 copy-start.2
  15.9 27.2 %spread.1 = (f32[512,512]{1,0:T(8,128)S(1)}, f32[512,1024]{1,0:T(8,128)S(1)}) custom-call(f32[512,1024]{1,0:T(8,128)S(1)} %copy-done.1), custom_call_target="tpu_custom_call" | custom-call | flops 1000000000 | bytes 10000000 | tf_op jit(solution)/shard_map/spread/pallas_call | solution.py:163
  43.1 0.0 copy-done.2
  43.1 0.0 copy-start.3
  43.1 43.5 %factor_rows.1 = (f32[512,1024]{1,0:T(8,128)}, f32[512,1024]{1,0:T(8,128)S(1)}) custom-call(f32[1]{0:T(128)} %bitcast.1.live, f32[512,512]{1,0:T(8,128)S(1)} %get-tuple-element.9.first, f32[512,1024]{1,0:T(8,128)S(1)} %get-tuple-element.10.second, f32[512,1024]{1,0:T(8,128)S(1)} %copy-done.2), custom_call_target="tpu_custom_call" | custom-call | flops 10000000000 | bytes 10000000 | tf_op jit(solution)/shard_map/factor_rows/pallas_call | solution.py:311
  86.6 43.5 %all-reduce.2.cloned.1.call-done.target = f32[512,1024]{1,0:T(8,128)} async-done(((f32[512,1024]{1,0:T(8,128)}), f32[512,1024]{1,0:T(8,128)}) %all-reduce.2.cloned.1.call-update) | async-done | bytes 2097168 | tf_op jit(solution)/shard_map/psum | solution.py:352
  130.1 0.0 copy-done.3
  130.2 0.0 copy-start
  130.2 1.6 %copy-done = f32[512,1024]{1,0:T(8,128)S(1)} copy-done((f32[512,1024]{1,0:T(8,128)S(1)}, f32[512,1024]{1,0:T(8,128)}, u32[]{:S(2)}) %copy-start) | copy-done | bytes 2097176
  131.7 2.8 %update_window.1 = f32[512,512]{1,0:T(8,128)} custom-call(f32[512,1024]{1,0:T(8,128)S(1)} %get-tuple-element.12.solved, f32[512,1024]{1,0:T(8,128)S(1)} %copy-done, f32[512,512]{1,0:T(8,128)S(1)} %copy-done.3), custom_call_target="tpu_custom_call" | custom-call | flops 1000000000 | bytes 10000000 | tf_op jit(solution)/shard_map/update_window/pallas_call | solution.py:334
Async XLA Ops:
  7.2 123.0 %all-reduce.2.cloned.1.call-start = ((), (), s32[]{:S(2)}) async-start(), calls=%async_computation | async-start | bytes 4194304 | tf_op jit(solution)/shard_map/psum | solution.py:352
  14.3 1.6 %copy-start.1 = (f32[512,1024]{1,0:T(8,128)S(1)}, f32[512,1024]{1,0:T(8,128)}, u32[]{:S(2)}) copy-start(f32[512,1024]{1,0:T(8,128)} %panel.1) | copy-start | bytes 6291460
  15.9 27.2 %copy-start.2 = (f32[512,1024]{1,0:T(8,128)S(1)}, f32[512,1024]{1,0:T(8,128)}, u32[]{:S(2)}) copy-start(f32[512,1024]{1,0:T(8,128)} %panel.1) | copy-start | bytes 6291460
  43.1 87.1 %copy-start.3 = (f32[512,512]{1,0:T(8,128)S(1)}, f32[512,512]{1,0:T(8,128)}, u32[]{:S(2)}) copy-start(f32[512,512]{1,0:T(8,128)} %window.1) | copy-start | bytes 3145732
  130.2 1.6 %copy-start = (f32[512,1024]{1,0:T(8,128)S(1)}, f32[512,1024]{1,0:T(8,128)}, u32[]{:S(2)}) copy-start(f32[512,1024]{1,0:T(8,128)} %all-reduce.2.cloned.1.call-done.target) | copy-start | bytes 6291460
Sparse Core Ops, SparseCore 0:
  14.4 115.6 all-reduce.1
